TPU v7x, 32 devices: a whole 2x2x4 slice. The times are simulated.
32 devices in a mesh: groups: 1, expert: 32 (over z, y, x, core), hidden: 1.
Axes of the slice: x: 2, y: 2, z: 4, core: 2. Of those that a mesh axis runs over, the one named last changes fastest.
Arguments:
- tokens: bfloat16 [512, 4096], P(('groups', 'expert')), may hold values from -6 to 6
- expert_ids: int32 [512, 8], P(('groups', 'expert')), may hold values from 0 to 15, all different within a row; in each aligned block of 16 rows (0 to 15, 16 to 31, ...) at most 16 rows name the same one
- router_scores: float32 [512, 8], P(('groups', 'expert')), may hold values from 0.05 to 1
- gate_weight: bfloat16 [32, 4096, 512], P('expert', None, 'hidden'), may hold values from -0.09375 to 0.09375
- up_weight: bfloat16 [32, 4096, 512], P('expert', None, 'hidden'), may hold values from -0.09375 to 0.09375
- down_weight: bfloat16 [32, 512, 4096], P('expert', 'hidden'), may hold values from -0.1875 to 0.1875
Outputs:
- moe_out: bfloat16 [512, 4096], P(('groups', 'expert'), 'hidden')
Inputs may be any that keep to these rules, and one draw needn't show every extreme that they name: `expert_ids`: each row names 8 different experts. In each aligned block of 16 rows no expert is named by more than 16 rows, a bound that some block reaches.
All inputs are finite; a program needn't handle non-finite values.
Results may differ from a plain program's by a relative error of at most 0.012.
Values may be sent and summed in bfloat16 or wider, within the bound.
A program may use at most 64 MiB of HBM per device.

v0:
```python
import jax
import jax.numpy as jnp
from jax import lax
from jax.sharding import PartitionSpec as P

SPAN = 2


def swapped(x, axis, bit):
    return lax.ppermute(x, axis, [(i, i ^ 1 << bit) for i in range(lax.axis_size(axis))])


def capacity(tok_count, top_count, expert_count):
    return max(2, min(tok_count, 2 * tok_count * top_count // expert_count))


def slot_numbers(expert_ids, expert_count, slot_cap):
    pair_ids = expert_ids.reshape(-1)
    onehot = (pair_ids[:, None] == jnp.arange(expert_count, dtype=jnp.int32)[None, :]).astype(
        jnp.int32
    )
    before = jnp.cumsum(onehot, axis=0) - onehot
    return pair_ids * slot_cap + jnp.sum(before * onehot, axis=1)


def expert_rows(received, gate_weight, up_weight, down_weight):
    source_count, row_count, model_width = received.shape
    row_block = received.reshape(source_count * row_count, model_width)
    gate_val = jnp.dot(row_block, gate_weight[0], preferred_element_type=jnp.float32)
    up_val = jnp.dot(row_block, up_weight[0], preferred_element_type=jnp.float32)
    activated = (jax.nn.silu(gate_val) * up_val).astype(jnp.bfloat16)
    pieces = jnp.dot(activated, down_weight[0], preferred_element_type=jnp.float32).astype(
        jnp.bfloat16
    )
    return pieces.reshape(source_count, row_count, model_width)


def body(tokens, expert_ids, router_scores, gate_weight, up_weight, down_weight):
    tok_count, model_width = tokens.shape
    top_count = expert_ids.shape[1]
    slots_all = lax.axis_size("expert")
    experts = slots_all // SPAN
    slot_cap = capacity(tok_count, top_count, experts)
    slot_index = slot_numbers(expert_ids, experts, slot_cap)
    token_of_pair = jnp.arange(tok_count * top_count, dtype=jnp.int32) // top_count
    owner_row = (
        jnp.full((experts * slot_cap,), tok_count, jnp.int32).at[slot_index].set(token_of_pair)
    )
    padded = jnp.concatenate([tokens, jnp.zeros((1, model_width), tokens.dtype)], axis=0)
    packed = padded[owner_row].reshape(experts, slot_cap, model_width)
    halves = packed.reshape(experts * SPAN, slot_cap // SPAN, model_width)
    own_half = lax.all_to_all(halves, "expert", split_axis=0, concat_axis=0, tiled=True)
    partner = swapped(own_half, "expert", 0)
    low_half = lax.axis_index("expert") % SPAN == 0
    received = jnp.where(
        low_half,
        jnp.concatenate([own_half, partner], axis=1),
        jnp.concatenate([partner, own_half], axis=1),
    )
    pieces = expert_rows(received, gate_weight, up_weight, down_weight)
    routed = 2.5 * router_scores / jnp.sum(router_scores, axis=1, keepdims=True)
    returned = lax.all_to_all(pieces, "expert", split_axis=0, concat_axis=0, tiled=True)
    combine_returned = returned.astype(jnp.float32)
    columns = combine_returned.shape[2]
    summed = jnp.sum(combine_returned.reshape(experts, SPAN, slot_cap, columns), axis=1).reshape(
        experts * slot_cap, columns
    )
    picked = summed[slot_index].reshape(tok_count, top_count, columns)
    mixed_rows = jnp.sum(routed[:, :, None] * picked, axis=1)
    result = lax.psum_scatter(
        mixed_rows.astype(jnp.bfloat16), "hidden", scatter_dimension=1, tiled=True
    )
    return result


def solution(mesh):
    return jax.shard_map(
        body,
        mesh=mesh,
        in_specs=(
            P(("groups", "expert"), None),
            P(("groups", "expert"), None),
            P(("groups", "expert"), None),
            P("expert", None, "hidden"),
            P("expert", None, "hidden"),
            P("expert", "hidden", None),
        ),
        out_specs=P(("groups", "expert"), "hidden"),
        check_vma=False,
    )
```

profile of v0, /device:TPU:0, one launch (start us, length us, event | category | flops | bytes accessed | tf_op | source)
XLA Modules:
  0.0 187.8 jit_solution(17367604682444048465)
XLA Ops:
  0.0 0.8 copy.12
  0.8 0.7 broadcast_multiply_fusion
  1.5 0.1 eq.21
  1.5 0.1 fusion.7
  1.6 0.2 reduce_window_sum.11
  1.8 0.2 select_reduce_fusion
  2.0 0.1 copy.11
  2.1 0.1 mul.45
  2.2 1.0 scatter_custom_fusion
  3.2 0.9 concatenate.9
  4.1 1.8 gather_fusion
  6.0 55.9 %all_to_all.10 = bf16[32,8,4096]{2,1,0:T(8,128)(2,1)} all-to-all(bf16[32,8,4096]{2,1,0:T(8,128)(2,1)S(1)} %bitcast.29), channel_id=1, replica_groups=mesh['groups'=1,'expert'=32,'hidden'=1] {'expert'}, dimensions={0} | all-to-all | bytes 4194304 | tf_op jit(solution)/shard_map/all_to_all | solution.py:52
  61.9 0.0 collective-permute-start
  61.9 0.0 copy-start.1
  61.9 4.4 %collective-permute-done = bf16[32,8,4096]{2,1,0:T(8,128)(2,1)S(1)} collective-permute-done((bf16[32,8,4096]{2,1,0:T(8,128)(2,1)}, bf16[32,8,4096]{2,1,0:T(8,128)(2,1)S(1)}, u32[]{:S(2)}, u32[]{:S(2)}) %collective-permute-start) | collective-permute-done | bytes 2097184 | tf_op jit(solution)/shard_map/ppermute | solution.py:10
  66.2 3.7 %maximum_select_fusion = bf16[32,16,4096]{2,1,0:T(8,128)(2,1)S(1)} fusion(bf16[32,8,4096]{2,1,0:T(8,128)(2,1)S(1)} %collective-permute-done, bf16[32,8,4096]{2,1,0:T(8,128)(2,1)} %all_to_all.10, pred[]{:T(512)S(6)} %eq.20), kind=kLoop, calls=%fused_computation.5 | loop fusion | flops 18874368 | bytes 8388609 | tf_op jit(solution)/shard_map/jit(_where)/select_n | solution.py:55
  70.0 0.0 copy-done.1
  70.0 0.0 copy-start.2
  70.0 2.3 %fusion.1 = f32[512,512]{1,0:T(8,128)S(1)} fusion(bf16[512,4096]{1,0:T(8,128)(2,1)S(1)} %bitcast.31, bf16[1,4096,512]{2,1,0:T(8,128)(2,1)S(1)} %copy-done.1), kind=kOutput, calls=%fused_computation.7 | convolution fusion | flops 2147483648 | bytes 9437184 | tf_op jit(solution)/shard_map/dot_general | solution.py:30
  72.3 0.0 copy-done.2
  72.3 0.0 copy-start.3
  72.3 2.3 %fusion.3 = f32[512,512]{1,0:T(8,128)S(1)} fusion(bf16[512,4096]{1,0:T(8,128)(2,1)S(1)} %bitcast.32, bf16[1,4096,512]{2,1,0:T(8,128)(2,1)S(1)} %copy-done.2), kind=kOutput, calls=%fused_computation.9 | convolution fusion | flops 2147483648 | bytes 9437184 | tf_op jit(solution)/shard_map/dot_general | solution.py:29
  74.7 0.0 copy-done.3
  74.7 4.3 %convolution_convert_fusion = bf16[512,4096]{1,0:T(8,128)(2,1)} fusion(bf16[1,512,4096]{2,1,0:T(8,128)(2,1)S(1)} %copy-done.3, f32[512,512]{1,0:T(8,128)S(1)} %fusion.1, f32[512,512]{1,0:T(8,128)S(1)} %fusion.3), kind=kOutput, calls=%fused_computation.4 | convolution fusion | flops 2151153664 | bytes 10485760 | tf_op jit(solution)/shard_map/dot_general | solution.py:32
  79.0 0.0 copy-start
  79.0 3.8 %all-to-all-start.1 = ((bf16[32,16,4096]{2,1,0:T(8,128)(2,1)}), bf16[32,16,4096]{2,1,0:T(8,128)(2,1)}, u32[]{:S(2)}, u32[]{:S(2)}) async-start(bf16[32,16,4096]{2,1,0:T(8,128)(2,1)} %bitcast.30), calls=%async_computation.1 | async-start | bytes 8388608 | tf_op jit(solution)/shard_map/all_to_all | solution.py:62
  82.8 0.0 copy-done
  82.9 0.1 copy.10
  82.9 93.6 %all-to-all-done.1 = bf16[32,16,4096]{2,1,0:T(8,128)(2,1)} async-done(((bf16[32,16,4096]{2,1,0:T(8,128)(2,1)}), bf16[32,16,4096]{2,1,0:T(8,128)(2,1)}, u32[]{:S(2)}, u32[]{:S(2)}) %all-to-all-start.1) | async-done | bytes 4194336 | tf_op jit(solution)/shard_map/all_to_all | solution.py:62
  176.5 5.5 %convert_reduce_fusion = f32[16,16,4096]{2,1,0:T(8,128)} fusion(bf16[32,16,4096]{2,1,0:T(8,128)(2,1)} %all-to-all-done.1), kind=kLoop, calls=%fused_computation.3 | loop fusion | flops 3145728 | bytes 8388608 | tf_op jit(solution)/shard_map/reduce_sum | solution.py:65
  182.0 4.4 %gather_fusion.1 = f32[128,4096]{1,0:T(8,128)S(1)} fusion(f32[256,4096]{1,0:T(8,128)} %bitcast.28, s32[1024]{0:T(1024)S(1)} %pad_clamp_fusion), kind=kCustom, calls=%fused_computation.1 | custom fusion | bytes 4194816 | tf_op jit(solution)/shard_map/gather | solution.py:68
  186.4 1.3 fusion.5
  (7 shorter events, 0.1 us)
Async XLA Ops:
  61.9 4.4 %collective-permute-start = (bf16[32,8,4096]{2,1,0:T(8,128)(2,1)}, bf16[32,8,4096]{2,1,0:T(8,128)(2,1)S(1)}, u32[]{:S(2)}, u32[]{:S(2)}) collective-permute-start(bf16[32,8,4096]{2,1,0:T(8,128)(2,1)} %all_to_all.10), channel_id=1, source_target_pairs={{0,1},{1,0},{2,3},{3,2},{4,5},{5,4},{6,7},{7,6},{8,9},{9,8},{10,11... | collective-permute-start | bytes 6291464 | tf_op jit(solution)/shard_map/ppermute | solution.py:10
  61.9 8.1 %copy-start.1 = (bf16[1,4096,512]{2,1,0:T(8,128)(2,1)S(1)}, bf16[1,4096,512]{2,1,0:T(8,128)(2,1)}, u32[]{:S(2)}) copy-start(bf16[1,4096,512]{2,1,0:T(8,128)(2,1)} %param.10) | copy-start | bytes 12582916
  70.0 2.3 %copy-start.2 = (bf16[1,4096,512]{2,1,0:T(8,128)(2,1)S(1)}, bf16[1,4096,512]{2,1,0:T(8,128)(2,1)}, u32[]{:S(2)}) copy-start(bf16[1,4096,512]{2,1,0:T(8,128)(2,1)} %param.9) | copy-start | bytes 12582916
  72.3 2.3 %copy-start.3 = (bf16[1,512,4096]{2,1,0:T(8,128)(2,1)S(1)}, bf16[1,512,4096]{2,1,0:T(8,128)(2,1)}, u32[]{:S(2)}) copy-start(bf16[1,512,4096]{2,1,0:T(8,128)(2,1)} %param.11) | copy-start | bytes 12582916
  79.0 3.8 %copy-start = (f32[16,8]{0,1:T(8,128)S(1)}, f32[16,8]{0,1:T(8,128)}, u32[]{:S(2)}) copy-start(f32[16,8]{0,1:T(8,128)} %param.8) | copy-start | bytes 1540
  79.0 97.5 %all-to-all-start.1 = ((bf16[32,16,4096]{2,1,0:T(8,128)(2,1)}), bf16[32,16,4096]{2,1,0:T(8,128)(2,1)}, u32[]{:S(2)}, u32[]{:S(2)}) async-start(bf16[32,16,4096]{2,1,0:T(8,128)(2,1)} %bitcast.30), calls=%async_computation.1 | async-start | bytes 8388608 | tf_op jit(solution)/shard_map/all_to_all | solution.py:62
where the time goes:
time: 188 us
  waiting for transfers between devices  97.9 us (52%)
  blocking collectives  55.9 us (30%)
  other arithmetic  11.7 us (6%)
  local copies, waits for them, and re-layouts  9.27 us (5%)
  matrix products  8.99 us (5%)
  starting transfers between devices  3.8 us (2%)
    all_to_all x1, waiting for transfers between devices, body(): lax.all_to_all(pieces, 'expert', split_axis=0, concat_axis=0, tiled=True)  93.6 us
    all_to_all x1, blocking collectives, body(): lax.all_to_all(halves, 'expert', split_axis=0, concat_axis=0, tiled=True)  55.9 us
    reduce_sum x1, other arithmetic, body(): jnp.sum(combine_returned.reshape(experts, SPAN, slot_cap, columns), axis=1)  5.5 us
    gather x1, local copies, waits for them, and re-layouts, body(): picked = summed[slot_index].reshape(tok_count, top_count, columns)  4.42 us
    ppermute x1, waiting for transfers between devices, swapped(): lax.ppermute(x, axis, [(i, i ^ 1 << bit) for i in range(lax.axis_size(axi...  4.37 us
    dot_general x1, matrix products, expert_rows(): jnp.dot(activated, down_weight[0], preferred_element_type=jnp.float32)  4.35 us
    all_to_all x1, starting transfers between devices, body(): lax.all_to_all(pieces, 'expert', split_axis=0, concat_axis=0, tiled=True)  3.8 us
  transfers between devices with their start and end apart: 2, of which 2 were waited for; matrix products, arithmetic and copies ran while one was open for 0% of the time, Pallas kernels for 0%

commit v1 on v0

v1 whole, which is shorter than its diff:
```python
import functools

import jax
import jax.numpy as jnp
from jax import lax
from jax.experimental import pallas as pl
from jax.experimental.pallas import tpu as pltpu
from jax.sharding import PartitionSpec as P

SPAN = 2
LANES = 128
MESH = pl.DeviceIdType.MESH


def ring_stages(ring):
    return [(d, 2 * d == ring) for d in range(1, ring // 2 + 1)]


def copy_count(ring):
    stages = len(ring_stages(ring))
    exchange = 2 * (4 + 2 * stages) + 4 * 2 * stages + 4 * ring
    return 2 * exchange + 8 * ring + 8


def layer_kernel(
    ring,
    experts,
    tok_hbm,
    ids_ref,
    scores_ref,
    gate_hbm,
    up_hbm,
    down_hbm,
    out_ref,
    rows_in,
    gate,
    up,
    down,
    act,
    terms,
    twin_in,
    az_in,
    ap_in,
    bp_in,
    bz_in,
    send_sem,
    recv_sem,
    local_sem,
):
    tok, width = out_ref.shape
    half_rows = ring * 4 * tok
    me = lax.axis_index("expert")
    core, plane, level = me % 2, (me // 2) % 4, me // 8
    px = plane + 1 - 2 * (plane % 2)
    py = plane + 2 - 4 * (plane // 2)
    pd = 3 - plane

    def device(zz, pp, cc):
        return zz * 8 + pp * 2 + cc

    def lev(step):
        return (level + step + ring) % ring

    dev_x, dev_y = device(level, px, core), device(level, py, core)
    dev_up, dev_dn = device(lev(1), plane, core), device(lev(-1), plane, core)
    twin = device(level, plane, 1 - core)

    def rows(zz, pp, cc=core):
        return pl.ds(pl.multiple_of((cc * (4 * ring) + zz * 4 + pp) * tok, tok), tok)

    quarter = width // 4
    wide = width + rows_in.shape[1] - width
    a_all, a_sub = pl.ds(0, 2 * quarter), (pl.ds(0, quarter), pl.ds(quarter, quarter))
    b_all = pl.ds(2 * quarter, wide - 2 * quarter)
    b_sub = (pl.ds(2 * quarter, quarter), pl.ds(3 * quarter, wide - 3 * quarter))
    stages = ring_stages(ring)

    loads = [
        pltpu.make_async_copy(tok_hbm, rows_in.at[rows(level, plane), pl.ds(0, width)], local_sem.at[0]),
        pltpu.make_async_copy(gate_hbm.at[0], gate, local_sem.at[1]),
        pltpu.make_async_copy(up_hbm.at[0], up, local_sem.at[2]),
        pltpu.make_async_copy(down_hbm.at[0], down, local_sem.at[3]),
    ]
    for load in loads:
        load.start()

    scores = scores_ref[...]
    routed = 2.5 * scores / jnp.sum(scores, axis=1, keepdims=True)
    ids = ids_ref[...]
    spare = wide - width
    lane = lax.broadcasted_iota(jnp.int32, (tok, spare), 1)
    table = jnp.zeros((tok, spare), jnp.float32)
    for k in range(ids.shape[1]):
        hit = (lane == ids[:, k : k + 1]) | (lane == ids[:, k : k + 1] + experts)
        table = table + jnp.where(hit, routed[:, k : k + 1], 0.0)
    high = table.astype(jnp.bfloat16).astype(jnp.float32)
    table = jnp.where(lane < experts, high, table - high)
    rows_in[rows(level, plane), pl.ds(width, spare)] = table.astype(jnp.bfloat16)

    barrier = pltpu.get_barrier_semaphore()
    friends = [twin, dev_x, dev_y] + ([dev_up, dev_dn] if ring > 1 else [])
    for friend in friends:
        pl.semaphore_signal(barrier, inc=1, device_id={"expert": friend}, device_id_type=MESH)
    loads[0].wait()
    pl.semaphore_wait(barrier, len(friends))

    sent = []

    def send(src, dst, target):
        number = len(sent)
        copy = pltpu.make_async_remote_copy(
            src_ref=src,
            dst_ref=dst,
            send_sem=send_sem.at[number],
            recv_sem=recv_sem.at[number],
            device_id={"expert": target},
            device_id_type=MESH,
        )
        copy.start()
        sent.append(copy)
        return copy

    def spread(zz, pp, cols, target):
        piece = rows_in.at[rows(zz, pp), cols]
        return send(piece, piece, target)

    from_twin = []

    def share(zz, pp, cols):
        from_twin.append(spread(zz, pp, cols, twin))

    def ring_send(stage, way, pp, cols, sub):
        d, split = stages[stage]
        step = -(d - 1) if way == 0 else d - 1
        return spread(lev(step), pp, sub[way] if split else cols, dev_up if way == 0 else dev_dn)

    def ring_start(pp, cols, sub):
        return [ring_send(0, way, pp, cols, sub) for way in (0, 1)] if stages else []

    def ring_step(stage, copies, pp, cols, sub, landed):
        d, split = stages[stage]
        later = []
        for way in (0, 1):
            copies[way].wait_recv()
            if stage + 1 < len(stages):
                later.append(ring_send(stage + 1, way, pp, cols, sub))
            if not split:
                landed(lev(-d if way == 0 else d))
        if split:
            landed(lev(d))
        return later

    def plane_start(zz, cols):
        return [spread(zz, plane, cols, dev_x), spread(zz, plane, cols, dev_y)]

    def plane_step(copies, zz, sub, landed):
        copies[0].wait_recv()
        later = [spread(zz, px, sub[0], dev_y)]
        landed(px)
        copies[1].wait_recv()
        later.append(spread(zz, py, sub[1], dev_x))
        landed(py)
        return later

    b_ring = ring_start(plane, b_all, b_sub)
    a_plane = plane_start(level, a_all)
    a_flows, b_flows = [], []

    def a_landed(pp):
        a_flows.append((pp, ring_start(pp, a_all, a_sub)))
        share(level, pp, a_all)

    def b_landed(zz):
        b_flows.append((zz, plane_start(zz, b_all)))
        share(zz, plane, b_all)

    a_landed(plane)
    b_landed(level)
    a_plane = plane_step(a_plane, level, a_sub, a_landed)
    for stage in range(len(stages)):
        b_ring = ring_step(stage, b_ring, plane, b_all, b_sub, b_landed)
    for copy in a_plane:
        copy.wait_recv()
    a_landed(pd)
    span = max(len(a_flows), len(b_flows))
    for i in range(span):
        if i < len(a_flows) and stages:
            pp, copies = a_flows[i]
            copies = ring_step(0, copies, pp, a_all, a_sub, lambda zz, pp=pp: share(zz, pp, a_all))
            a_flows[i] = (pp, copies)
        if i < len(b_flows):
            zz, copies = b_flows[i]
            b_flows[i] = (
                zz,
                plane_step(copies, zz, b_sub, lambda pp, zz=zz: share(zz, pp, b_all)),
            )
    for stage in range(1, len(stages)):
        for i in range(len(a_flows)):
            pp, copies = a_flows[i]
            copies = ring_step(
                stage, copies, pp, a_all, a_sub, lambda zz, pp=pp: share(zz, pp, a_all)
            )
            a_flows[i] = (pp, copies)
    for zz, copies in b_flows:
        for copy in copies:
            copy.wait_recv()
        share(zz, pd, b_all)
    for load in loads[1:]:
        load.wait()

    def hidden_units(first):
        block = pl.ds(pl.multiple_of(first, tok), half_rows)
        gate_val = jnp.dot(rows_in[block, pl.ds(0, width)], gate[...], preferred_element_type=jnp.float32)
        up_val = jnp.dot(rows_in[block, pl.ds(0, width)], up[...], preferred_element_type=jnp.float32)
        act[block, :] = (jax.nn.silu(gate_val) * up_val).astype(jnp.bfloat16)

    def share_of(first):
        block = pl.ds(pl.multiple_of(first, tok), half_rows)
        entry = rows_in[block, pl.ds(width, spare)].astype(jnp.float32)
        place = lax.broadcasted_iota(jnp.int32, entry.shape, 1)
        mine = me // SPAN
        hit = (place == mine) | (place == mine + experts)
        return jnp.sum(jnp.where(hit, entry, 0.0), axis=1, keepdims=True)

    own_first, twin_first = core * half_rows, (1 - core) * half_rows
    hidden_units(own_first)
    for copy in from_twin:
        copy.wait_recv()
    hidden_units(twin_first)

    weight = share_of(twin_first)
    twin_block = pl.ds(pl.multiple_of(twin_first, tok), half_rows)
    own_block = pl.ds(pl.multiple_of(own_first, tok), half_rows)
    swaps = []
    for q in range(4):
        cols = pl.ds(q * quarter, quarter)
        piece = jnp.dot(act[twin_block, :], down[:, cols], preferred_element_type=jnp.float32)
        terms[twin_block, cols] = (weight * piece).astype(jnp.bfloat16)
        swaps.append(send(terms.at[twin_block, cols], twin_in.at[q], twin))
    weight = share_of(own_first)
    for q in range(4):
        cols = pl.ds(q * quarter, quarter)
        piece = jnp.dot(act[own_block, :], down[:, cols], preferred_element_type=jnp.float32)
        swaps[q].wait_recv()
        total = weight * piece + twin_in[q].astype(jnp.float32)
        terms[own_block, cols] = total.astype(jnp.bfloat16)

    c_all, c_sub = pl.ds(2 * quarter, 2 * quarter), tuple(pl.ds(i * quarter, quarter) for i in (2, 3))

    def add(zz, pp, cols, *arrived):
        block = terms[rows(zz, pp), cols].astype(jnp.float32)
        for piece in arrived:
            block = block + piece.astype(jnp.float32)
        terms[rows(zz, pp), cols] = block.astype(jnp.bfloat16)

    def local(cols, start):
        return pl.ds(cols.start - start, cols.size)

    def fold_send(stage, way, pp, cols, sub, inbox):
        d, split = stages[stage]
        part = sub[way] if split else cols
        return send(
            terms.at[rows(lev(d if way == 0 else -d), pp), part],
            inbox.at[way, stage, :, local(part, cols.start)],
            dev_up if way == 0 else dev_dn,
        )

    def fold_start(pp, cols, sub, inbox):
        return [fold_send(len(stages) - 1, way, pp, cols, sub, inbox) for way in (0, 1)] if stages else []

    def fold_down(copies, pp, cols, sub, inbox):
        for stage in range(len(stages) - 1, 0, -1):
            d, split = stages[stage]
            later = []
            for way in (0, 1):
                part = sub[way] if split else cols
                copies[way].wait_recv()
                add(lev(d - 1 if way == 0 else 1 - d), pp, part, inbox[way, stage, :, local(part, cols.start)])
                later.append(fold_send(stage - 1, way, pp, cols, sub, inbox))
            copies = later
        return copies

    def fold_last(copies, pp, cols, sub, inbox):
        if not stages:
            return
        for copy in copies:
            copy.wait_recv()
        if stages[0][1]:
            for way in (0, 1):
                add(level, pp, sub[way], inbox[way, 0, :, local(sub[way], cols.start)])
        else:
            add(level, pp, cols, inbox[0, 0], inbox[1, 0])

    def cross_start(zz, cols, sub, inbox):
        return [
            send(terms.at[rows(zz, pd), sub[i]], inbox.at[i, 0, :, local(sub[i], cols.start)], target)
            for i, target in ((0, dev_x), (1, dev_y))
        ]

    def cross_down(copies, zz, cols, sub, inbox):
        copies[0].wait_recv()
        add(zz, py, sub[0], inbox[0, 0, :, local(sub[0], cols.start)])
        to_y = send(terms.at[rows(zz, py), cols], inbox.at[1, 1], dev_y)
        copies[1].wait_recv()
        add(zz, px, sub[1], inbox[1, 0, :, local(sub[1], cols.start)])
        to_x = send(terms.at[rows(zz, px), cols], inbox.at[0, 1], dev_x)
        return [to_y, to_x]

    planes = [pd, px, py, plane]
    levels = []
    for d, split in reversed(stages):
        levels += [lev(d)] if split else [lev(d), lev(-d)]
    if ring % 2 == 1 and ring > 1 and not levels:
        levels = []
    levels.append(level)
    a_fold = [fold_start(planes[j], a_all, a_sub, az_in.at[j]) for j in range(4)]
    b_cross = [cross_start(levels[i], c_all, c_sub, bp_in.at[i]) for i in range(len(levels))]
    for i in range(max(4, len(levels))):
        if i < 4:
            a_fold[i] = fold_down(a_fold[i], planes[i], a_all, a_sub, az_in.at[i])
        if i < len(levels):
            b_cross[i] = cross_down(b_cross[i], levels[i], c_all, c_sub, bp_in.at[i])
    a_cross, b_fold = None, None
    for i in range(max(4, len(levels))):
        if i < 4:
            fold_last(a_fold[i], planes[i], a_all, a_sub, az_in.at[i])
            if i == 0:
                a_cross = cross_start(level, a_all, a_sub, ap_in)
        if i < len(levels):
            for copy in b_cross[i]:
                copy.wait_recv()
            add(levels[i], plane, c_all, bp_in[i, 0, 1], bp_in[i, 1, 1])
            if i == (0 if stages and stages[-1][1] else min(1, len(levels) - 1)):
                b_fold = fold_start(plane, c_all, c_sub, bz_in)
        if i == 2:
            a_cross = cross_down(a_cross, level, a_all, a_sub, ap_in)
    b_fold = fold_down(b_fold, plane, c_all, c_sub, bz_in)
    for copy in a_cross:
        copy.wait_recv()
    out_ref[:, a_all] = (
        terms[rows(level, plane), a_all].astype(jnp.float32)
        + ap_in[0, 1].astype(jnp.float32)
        + ap_in[1, 1].astype(jnp.float32)
    ).astype(jnp.bfloat16)
    fold_last(b_fold, plane, c_all, c_sub, bz_in)
    out_ref[:, c_all] = terms[rows(level, plane), c_all]
    for copy in sent:
        copy.wait_send()


def body(ring, tokens, expert_ids, router_scores, gate_weight, up_weight, down_weight):
    tok, width = tokens.shape
    hidden = gate_weight.shape[2]
    slots = lax.axis_size("expert")
    experts = slots // SPAN
    spare = -(-2 * experts // LANES) * LANES
    all_rows, half = slots * tok, width // 2
    depth = max(1, len(ring_stages(ring)))
    bf16 = jnp.bfloat16
    anywhere = pl.BlockSpec(memory_space=pl.ANY)
    vmem = pl.BlockSpec(memory_space=pltpu.VMEM)
    mixed = pl.pallas_call(
        functools.partial(layer_kernel, ring, experts),
        out_shape=jax.ShapeDtypeStruct((tok, width), bf16),
        in_specs=[anywhere, vmem, vmem, anywhere, anywhere, anywhere],
        out_specs=vmem,
        scratch_shapes=[
            pltpu.VMEM((all_rows, width + spare), bf16),
            pltpu.VMEM((width, hidden), bf16),
            pltpu.VMEM((width, hidden), bf16),
            pltpu.VMEM((hidden, width), bf16),
            pltpu.VMEM((all_rows, hidden), bf16),
            pltpu.VMEM((all_rows, width), bf16),
            pltpu.VMEM((4, all_rows // 2, width // 4), bf16),
            pltpu.VMEM((4, 2, depth, tok, half), bf16),
            pltpu.VMEM((2, 2, tok, half), bf16),
            pltpu.VMEM((ring, 2, 2, tok, half), bf16),
            pltpu.VMEM((2, depth, tok, half), bf16),
            pltpu.SemaphoreType.DMA((copy_count(ring),)),
            pltpu.SemaphoreType.DMA((copy_count(ring),)),
            pltpu.SemaphoreType.DMA((4,)),
        ],
        compiler_params=pltpu.CompilerParams(
            collective_id=0, has_side_effects=True, vmem_limit_bytes=60 << 20
        ),
    )(tokens, expert_ids, router_scores, gate_weight, up_weight, down_weight)
    if lax.axis_size("hidden") == 1:
        return mixed
    return lax.psum_scatter(mixed, "hidden", scatter_dimension=1, tiled=True)


def solution(mesh):
    return jax.shard_map(
        functools.partial(body, mesh.shape["expert"] // 8),
        mesh=mesh,
        in_specs=(
            P(("groups", "expert"), None),
            P(("groups", "expert"), None),
            P(("groups", "expert"), None),
            P("expert", None, "hidden"),
            P("expert", None, "hidden"),
            P("expert", "hidden", None),
        ),
        out_specs=P(("groups", "expert"), "hidden"),
        check_vma=False,
    )
```

time: 188 us -> 72.9 us (0.39)
  waiting for transfers between devices: 97.9 us -> 0 us
  Pallas kernels: 0 us -> 68.3 us
  blocking collectives: 55.9 us -> 0 us
  other arithmetic: 11.7 us -> 0 us
  matrix products: 8.99 us -> 0 us
  local copies, waits for them, and re-layouts: 9.27 us -> 4.27 us
  starting transfers between devices: 3.8 us -> 0 us
    all_to_all x1 -> x0, waiting for transfers between devices: 93.6 us -> none  [body(): lax.all_to_all(pieces, 'expert', split_axis=0, concat_axis=0, tiled=True)]
    pallas_call x0 -> x1, Pallas kernels: none -> 68.3 us  [body(): pl.pallas_call(functools.partial(layer_kernel, ring, experts), out_shape=...]
    all_to_all x1 -> x0, blocking collectives: 55.9 us -> none  [body(): lax.all_to_all(halves, 'expert', split_axis=0, concat_axis=0, tiled=True)]
    dot_general x3 -> x0, matrix products: 8.99 us -> none  [the longest x1 4.35 us: expert_rows(): jnp.dot(activated, down_weight[0], preferred_element_type=jnp.float32)]
    reduce_sum x4 -> x0, other arithmetic: 7.03 us -> none  [the longest x1 5.5 us: body(): jnp.sum(combine_returned.reshape(experts, SPAN, slot_cap, columns), axis=1)]
    gather x2 -> x0, local copies, waits for them, and re-layouts: 6.27 us -> none  [the longest x1 4.42 us: body(): picked = summed[slot_index].reshape(tok_count, top_count, columns)]
    ppermute x1 -> x0, waiting for transfers between devices: 4.37 us -> none  [swapped(): lax.ppermute(x, axis, [(i, i ^ 1 << bit) for i in range(lax.axis_size(axi...]
    all_to_all x1 -> x0, starting transfers between devices: 3.8 us -> none  [body(): lax.all_to_all(pieces, 'expert', split_axis=0, concat_axis=0, tiled=True)]
  transfers between devices with their start and end apart: 2 -> 0, of which waited for: 2 -> 0; matrix products, arithmetic and copies ran while one was open for 0% -> 0% of each run, Pallas kernels for 0% -> 0%
where the time goes in v1:
time: 72.9 us; the launch traced here: 72.6 us
  Pallas kernels  68.3 us (94%)
  local copies, waits for them, and re-layouts  4.27 us (6%)
    pallas_call x1, Pallas kernels, body(): pl.pallas_call(functools.partial(layer_kernel, ring, experts), out_shape=...  68.3 us
    unnamed x3, local copies, waits for them, and re-layouts  4.27 us

profile of v1, /device:TPU:0, one launch (start us, length us, event | category | flops | bytes accessed | tf_op | source)
XLA Modules:
  0.0 72.6 jit_solution(2975412627138451341)
XLA Ops:
  0.0 1.4 %copy.7.ids_ref = s32[16,8]{1,0:T(8,128)} copy(s32[16,8]{0,1:T(8,128)} %param.7) | data formatting | bytes 1024 | tf_op args[1]
  1.4 1.4 %copy.8.scores_ref = f32[16,8]{1,0:T(8,128)} copy(f32[16,8]{0,1:T(8,128)} %param.8) | data formatting | bytes 1024 | tf_op args[2]
  2.7 68.3 %shard_map.64 = bf16[16,4096]{1,0:T(8,128)(2,1)} custom-call(bf16[16,4096]{1,0:T(8,128)(2,1)} %tok_hbm.1, s32[16,8]{1,0:T(8,128)} %copy.7.ids_ref, f32[16,8]{1,0:T(8,128)} %copy.8.scores_ref, bf16[1,4096,512]{2,1,0:T(8,128)(2,1)} %gate_hbm.1, bf16[1,4096,512]{2,1,0:T(8,128)(2,1)} %up_hbm.1, bf16[1,512,4096]{2,1,0:T(8,128)(2,1)} %down_hbm.1), custom_call_target="tpu_custom_call" | custom-call | tf_op jit(solution)/shard_map/pallas_call | solution.py:362
  71.0 1.6 %copy.10 = bf16[16,4096]{1,0:T(8,128)(2,1)} copy(bf16[16,4096]{1,0:T(8,128)(2,1)} %shard_map.64) | data formatting | bytes 262144

commit v2 on v1

v2 whole, which is shorter than its diff:
```python
import functools

import jax
import jax.numpy as jnp
from jax import lax
from jax.experimental import pallas as pl
from jax.experimental.pallas import tpu as pltpu
from jax.sharding import PartitionSpec as P

SPAN = 2
LANES = 128
MESH = pl.DeviceIdType.MESH


def copy_count(ring):
    exchange = 8 * (ring - 1) + 4 + 2 * (ring - 1) + 4 * (2 * ring - 1)
    return 2 * exchange + 16 * ring + 8


def layer_kernel(
    ring,
    experts,
    tok_hbm,
    ids_ref,
    scores_ref,
    gate_hbm,
    up_hbm,
    down_hbm,
    out_ref,
    rows_in,
    gate,
    up,
    down,
    act,
    terms,
    twin_in,
    az_in,
    ap_in,
    bp_in,
    bz_in,
    send_sem,
    recv_sem,
    local_sem,
):
    tok, width = out_ref.shape
    half_rows = ring * 4 * tok
    me = lax.axis_index("expert")
    core, plane, level = me % 2, (me // 2) % 4, me // 8
    px = plane + 1 - 2 * (plane % 2)
    py = plane + 2 - 4 * (plane // 2)
    pd = 3 - plane

    def device(zz, pp, cc):
        return zz * 8 + pp * 2 + cc

    def lev(step):
        return (level + step + ring) % ring

    def inside(step):
        return (level + step >= 0) & (level + step < ring)

    dev_x, dev_y = device(level, px, core), device(level, py, core)
    ways = (1, -1)
    next_dev = [device(lev(way), plane, core) for way in ways]
    twin = device(level, plane, 1 - core)

    def rows(zz, pp, cc=core):
        return pl.ds(pl.multiple_of((cc * (4 * ring) + zz * 4 + pp) * tok, tok), tok)

    quarter = width // 4
    wide = rows_in.shape[1]
    edge = quarter + 3 * quarter // 2
    a_all, a_sub = pl.ds(0, quarter), (pl.ds(0, quarter // 2), pl.ds(quarter // 2, quarter // 2))
    b_all = pl.ds(quarter, wide - quarter)
    b_sub = (pl.ds(quarter, edge - quarter), pl.ds(edge, wide - edge))
    c_all = pl.ds(quarter, width - quarter)
    c_sub = (pl.ds(quarter, edge - quarter), pl.ds(edge, width - edge))

    loads = [
        pltpu.make_async_copy(tok_hbm, rows_in.at[rows(level, plane), pl.ds(0, width)], local_sem.at[0]),
        pltpu.make_async_copy(gate_hbm.at[0], gate, local_sem.at[1]),
        pltpu.make_async_copy(up_hbm.at[0], up, local_sem.at[2]),
        pltpu.make_async_copy(down_hbm.at[0], down, local_sem.at[3]),
    ]
    for load in loads:
        load.start()

    scores = scores_ref[...]
    routed = 2.5 * scores / jnp.sum(scores, axis=0, keepdims=True)
    ids = ids_ref[...]
    spare = wide - width
    entry = lax.broadcasted_iota(jnp.int32, (spare, tok), 0)
    table = jnp.zeros((spare, tok), jnp.float32)
    for k in range(ids.shape[0]):
        hit = (entry == ids[k : k + 1]) | (entry == ids[k : k + 1] + experts)
        table = table + jnp.where(hit, routed[k : k + 1], 0.0)
    high = table.astype(jnp.bfloat16).astype(jnp.float32)
    table = jnp.where(entry < experts, high, table - high)
    rows_in[rows(level, plane), pl.ds(width, spare)] = table.T.astype(jnp.bfloat16)

    barrier = pltpu.get_barrier_semaphore()
    def greet(friend):
        pl.semaphore_signal(barrier, inc=1, device_id={"expert": friend}, device_id_type=MESH)

    for friend in (twin, dev_x, dev_y):
        greet(friend)
    for way, friend in zip(ways, next_dev):
        pl.when(inside(way))(functools.partial(greet, friend))
    loads[0].wait()
    pl.semaphore_wait(barrier, 3 + sum(inside(way).astype(jnp.int32) for way in ways))

    sent = []

    def plan(src, dst, target, leaves=None):
        number = len(sent)
        copy = pltpu.make_async_remote_copy(
            src_ref=src,
            dst_ref=dst,
            send_sem=send_sem.at[number],
            recv_sem=recv_sem.at[number],
            device_id={"expert": target},
            device_id_type=MESH,
        )
        sent.append((copy, leaves))
        return copy

    def send(src, dst, target):
        copy = plan(src, dst, target)
        copy.start()
        return copy

    def spread(zz, pp, cols, target, leaves=None):
        piece = rows_in.at[rows(zz, pp), cols]
        return plan(piece, piece, target, leaves)

    from_twin = []

    def share(zz, pp, cols, there=None):
        copy = spread(zz, pp, cols, twin, there)
        from_twin.append((copy, there))
        return copy

    def line(pp, cols):
        return [
            [
                spread(lev(-way * (d - 1)), pp, cols, next_dev[i], inside(-way * (d - 1)) & inside(way))
                for i, way in enumerate(ways)
            ]
            for d in range(1, ring)
        ]

    def start_line(flow):
        for i, way in enumerate(ways):
            if flow:
                pl.when(inside(way))(flow[0][i].start)

    def step_line(flow, d, i, after):
        way = ways[i]

        @pl.when(inside(-way * d))
        def _():
            flow[d - 1][i].wait_recv()
            if d < ring - 1:
                pl.when(inside(way))(flow[d][i].start)
            for copy in after:
                copy.start()

    def cross(zz, cols, sub, there=None):
        return [
            spread(zz, plane, cols, dev_x, there),
            spread(zz, plane, cols, dev_y, there),
            spread(zz, px, sub[0], dev_y, there),
            spread(zz, py, sub[1], dev_x, there),
        ]

    b_line = line(plane, b_all)
    a_cross = cross(level, a_all, a_sub)
    a_lines = {name: line(pp, a_all) for name, pp in (("own", plane), ("x", px), ("y", py), ("d", pd))}
    a_place = {"own": plane, "x": px, "y": py, "d": pd}
    b_flows = []

    start_line(b_line)
    a_cross[0].start()
    a_cross[1].start()

    def open_cross(zz, there=None):
        copies = cross(zz, b_all, b_sub, there)
        b_flows.append((zz, there, copies))
        return [copies[0], copies[1], share(zz, plane, b_all, there)]

    for copy in open_cross(level):
        copy.start()
    start_line(a_lines["own"])
    share(level, plane, a_all).start()
    for i, name in enumerate(("x", "y")):
        a_cross[i].wait_recv()
        a_cross[2 + i].start()
        start_line(a_lines[name])
        share(level, a_place[name], a_all).start()
    for i, way in enumerate(ways):
        if ring > 1:
            step_line(b_line, 1, i, open_cross(lev(-way), inside(-way)))
    a_cross[2].wait_recv()
    a_cross[3].wait_recv()
    start_line(a_lines["d"])
    share(level, pd, a_all).start()

    def step_cross(flow):
        zz, there, copies = flow
        shares = [share(zz, px, b_all, there), share(zz, py, b_all, there)]

        def act():
            for i in (0, 1):
                copies[i].wait_recv()
                copies[2 + i].start()
                shares[i].start()

        act() if there is None else pl.when(there)(act)

    def end_cross(flow):
        zz, there, copies = flow
        last = share(zz, pd, b_all, there)

        def act():
            copies[2].wait_recv()
            copies[3].wait_recv()
            last.start()

        act() if there is None else pl.when(there)(act)

    def step_a(d):
        for name, flow in a_lines.items():
            for i, way in enumerate(ways):
                there = inside(-way * d)
                step_line(flow, d, i, [share(lev(-way * d), a_place[name], a_all, there)])

    step_cross(b_flows[0])
    for d in range(1, ring):
        if d + 1 < ring:
            for i, way in enumerate(ways):
                step_line(b_line, d + 1, i, open_cross(lev(-way * (d + 1)), inside(-way * (d + 1))))
        for flow in b_flows[max(0, 2 * d - 3) : 2 * d - 1]:
            end_cross(flow)
        step_cross(b_flows[2 * d - 1])
        step_cross(b_flows[2 * d])
        step_a(d)
    for flow in b_flows[max(0, 2 * ring - 3) :]:
        end_cross(flow)
    for load in loads[1:]:
        load.wait()

    def hidden_units(first):
        block = pl.ds(pl.multiple_of(first, tok), half_rows)
        gate_val = jnp.dot(rows_in[block, pl.ds(0, width)], gate[...], preferred_element_type=jnp.float32)
        up_val = jnp.dot(rows_in[block, pl.ds(0, width)], up[...], preferred_element_type=jnp.float32)
        act[block, :] = (jax.nn.silu(gate_val) * up_val).astype(jnp.bfloat16)

    def share_of(first):
        block = pl.ds(pl.multiple_of(first, tok), half_rows)
        entry = rows_in[block, pl.ds(width, spare)].astype(jnp.float32)
        place = lax.broadcasted_iota(jnp.int32, entry.shape, 1)
        mine = me // SPAN
        hit = (place == mine) | (place == mine + experts)
        return jnp.sum(jnp.where(hit, entry, 0.0), axis=1, keepdims=True)

    own_first, twin_first = core * half_rows, (1 - core) * half_rows
    hidden_units(own_first)
    for copy, there in from_twin:
        copy.wait_recv() if there is None else pl.when(there)(copy.wait_recv)
    hidden_units(twin_first)

    weight = share_of(twin_first)
    twin_block = pl.ds(pl.multiple_of(twin_first, tok), half_rows)
    own_block = pl.ds(pl.multiple_of(own_first, tok), half_rows)
    swaps = []
    for q in range(4):
        cols = pl.ds(q * quarter, quarter)
        piece = jnp.dot(act[twin_block, :], down[:, cols], preferred_element_type=jnp.float32)
        terms[twin_block, cols] = (weight * piece).astype(jnp.bfloat16)
        swaps.append(send(terms.at[twin_block, cols], twin_in.at[q], twin))
    weight = share_of(own_first)
    for q in range(4):
        cols = pl.ds(q * quarter, quarter)
        piece = jnp.dot(act[own_block, :], down[:, cols], preferred_element_type=jnp.float32)
        swaps[q].wait_recv()
        total = weight * piece + twin_in[q].astype(jnp.float32)
        terms[own_block, cols] = total.astype(jnp.bfloat16)

    def add(zz, pp, cols, *arrived):
        block = terms[rows(zz, pp), cols].astype(jnp.float32)
        for piece in arrived:
            block = block + piece.astype(jnp.float32)
        terms[rows(zz, pp), cols] = block.astype(jnp.bfloat16)

    def local(cols, start):
        return pl.ds(cols.start - start, cols.size)

    def fold(pp, cols, inbox):
        return [
            [
                plan(terms.at[rows(lev(way * d), pp), cols], inbox.at[i, d - 1], next_dev[i], inside(way * d))
                for i, way in enumerate(ways)
            ]
            for d in range(1, ring)
        ]

    def fold_start(flow):
        for i, way in enumerate(ways):
            if flow:
                pl.when(inside(way * (ring - 1)))(flow[-1][i].start)

    def fold_step(flow, d, pp, cols, inbox):
        for i, way in enumerate(ways):

            @pl.when(inside(-way) & inside(way * (d - 1)))
            def _():
                flow[d - 1][i].wait_recv()
                add(lev(way * (d - 1)), pp, cols, inbox[i, d - 1])

            if d > 1:
                pl.when(inside(way * (d - 1)))(flow[d - 2][i].start)

    def cross_start(zz, cols, sub, inbox):
        return [
            send(terms.at[rows(zz, pd), sub[i]], inbox.at[i, 0, :, local(sub[i], cols.start)], target)
            for i, target in ((0, dev_x), (1, dev_y))
        ]

    def cross_down(copies, zz, cols, sub, inbox):
        copies[0].wait_recv()
        add(zz, py, sub[0], inbox[0, 0, :, local(sub[0], cols.start)])
        to_y = send(terms.at[rows(zz, py), cols], inbox.at[1, 1], dev_y)
        copies[1].wait_recv()
        add(zz, px, sub[1], inbox[1, 0, :, local(sub[1], cols.start)])
        to_x = send(terms.at[rows(zz, px), cols], inbox.at[0, 1], dev_x)
        return [to_y, to_x]

    planes = [pd, px, py, plane]
    levels = [zz for i in range(ring // 2) for zz in (ring - 1 - i, i)] + [ring // 2] * (ring % 2)
    a_fold = [fold(pp, a_all, az_in.at[j]) for j, pp in enumerate(planes)]
    b_fold = fold(plane, c_all, bz_in)
    b_cross = [cross_start(zz, c_all, c_sub, bp_in.at[i]) for i, zz in enumerate(levels)]
    for flow in a_fold:
        fold_start(flow)

    def a_step(d, j):
        fold_step(a_fold[j], d, planes[j], a_all, az_in.at[j])

    def b_down(i):
        b_cross[i] = cross_down(b_cross[i], levels[i], c_all, c_sub, bp_in.at[i])

    def b_sum(i):
        for copy in b_cross[i]:
            copy.wait_recv()
        add(levels[i], plane, c_all, bp_in[i, 0, 1], bp_in[i, 1, 1])
        if i == min(1, ring - 1):
            fold_start(b_fold)

    b_work = []
    for i in range(ring):
        b_work.append(functools.partial(b_down, i))
        if i > 0:
            b_work.append(functools.partial(b_sum, i - 1))
    b_work.append(functools.partial(b_sum, ring - 1))
    a_work = [functools.partial(a_step, d, j) for d in range(ring - 1, 0, -1) for j in range(4)]
    for i in range(max(len(a_work), len(b_work))):
        if i * len(b_work) // len(a_work or b_work) != (i + 1) * len(b_work) // len(a_work or b_work):
            b_work[i * len(b_work) // len(a_work or b_work)]()
        if i < len(a_work):
            a_work[i]()
    a_cross = cross_start(level, a_all, a_sub, ap_in)
    a_cross = cross_down(a_cross, level, a_all, a_sub, ap_in)
    for d in range(ring - 1, 0, -1):
        fold_step(b_fold, d, plane, c_all, bz_in)
    for copy in a_cross:
        copy.wait_recv()
    add(level, plane, a_all, ap_in[0, 1], ap_in[1, 1])
    out_ref[...] = terms[rows(level, plane), :]
    for copy, leaves in sent:
        copy.wait_send() if leaves is None else pl.when(leaves)(copy.wait_send)


def body(ring, tokens, expert_ids, router_scores, gate_weight, up_weight, down_weight):
    tok, width = tokens.shape
    hidden = gate_weight.shape[2]
    slots = lax.axis_size("expert")
    experts = slots // SPAN
    spare = -(-2 * experts // LANES) * LANES
    all_rows, narrow, broad = slots * tok, width // 4, width - width // 4
    depth = max(1, ring - 1)
    bf16 = jnp.bfloat16
    anywhere = pl.BlockSpec(memory_space=pl.ANY)
    vmem = pl.BlockSpec(memory_space=pltpu.VMEM)
    mixed = pl.pallas_call(
        functools.partial(layer_kernel, ring, experts),
        out_shape=jax.ShapeDtypeStruct((tok, width), bf16),
        in_specs=[anywhere, vmem, vmem, anywhere, anywhere, anywhere],
        out_specs=vmem,
        scratch_shapes=[
            pltpu.VMEM((all_rows, width + spare), bf16),
            pltpu.VMEM((width, hidden), bf16),
            pltpu.VMEM((width, hidden), bf16),
            pltpu.VMEM((hidden, width), bf16),
            pltpu.VMEM((all_rows, hidden), bf16),
            pltpu.VMEM((all_rows, width), bf16),
            pltpu.VMEM((4, all_rows // 2, width // 4), bf16),
            pltpu.VMEM((4, 2, depth, tok, narrow), bf16),
            pltpu.VMEM((2, 2, tok, narrow), bf16),
            pltpu.VMEM((ring, 2, 2, tok, broad), bf16),
            pltpu.VMEM((2, depth, tok, broad), bf16),
            pltpu.SemaphoreType.DMA((copy_count(ring),)),
            pltpu.SemaphoreType.DMA((copy_count(ring),)),
            pltpu.SemaphoreType.DMA((4,)),
        ],
        compiler_params=pltpu.CompilerParams(
            collective_id=0, has_side_effects=True, vmem_limit_bytes=60 << 20
        ),
    )(tokens, expert_ids.T, router_scores.T, gate_weight, up_weight, down_weight)
    if lax.axis_size("hidden") == 1:
        return mixed
    return lax.psum_scatter(mixed, "hidden", scatter_dimension=1, tiled=True)


def solution(mesh):
    return jax.shard_map(
        functools.partial(body, mesh.shape["expert"] // 8),
        mesh=mesh,
        in_specs=(
            P(("groups", "expert"), None),
            P(("groups", "expert"), None),
            P(("groups", "expert"), None),
            P("expert", None, "hidden"),
            P("expert", None, "hidden"),
            P("expert", "hidden", None),
        ),
        out_specs=P(("groups", "expert"), "hidden"),
        check_vma=False,
    )
```

time: 72.9 us -> 68.1 us (0.934)
  local copies, waits for them, and re-layouts: 4.27 us -> 1.57 us
  Pallas kernels: 68.3 us -> 66.3 us
    unnamed x3 -> x1, local copies, waits for them, and re-layouts: 4.27 us -> 1.57 us
    pallas_call x1, Pallas kernels: 68.3 us -> 66.3 us  [body(): pl.pallas_call(functools.partial(layer_kernel, ring, experts), out_shape=...]
where the time goes in v2:
time: 68.1 us; the launch traced here: 67.9 us
  Pallas kernels  66.3 us (97%)
  local copies, waits for them, and re-layouts  1.57 us (2%)
    pallas_call x1, Pallas kernels, body(): pl.pallas_call(functools.partial(layer_kernel, ring, experts), out_shape=...  66.3 us
    unnamed x1, local copies, waits for them, and re-layouts  1.57 us

profile of v2, /device:TPU:0, one launch (start us, length us, event | category | flops | bytes accessed | tf_op | source)
XLA Modules:
  0.0 67.9 jit_solution(14661455750667081931)
XLA Ops:
  0.0 66.3 %shard_map.64 = bf16[16,4096]{1,0:T(8,128)(2,1)} custom-call(bf16[16,4096]{1,0:T(8,128)(2,1)} %tok_hbm.1, s32[8,16]{1,0:T(8,128)} %bitcast.2, f32[8,16]{1,0:T(8,128)} %bitcast.3, bf16[1,4096,512]{2,1,0:T(8,128)(2,1)} %gate_hbm.1, bf16[1,4096,512]{2,1,0:T(8,128)(2,1)} %up_hbm.1, bf16[1,512,4096]{2,1,0:T(8,128)(2,1)} %down_hbm.1), custom_call_target="tpu_custom_call" | custom-call | tf_op jit(solution)/shard_map/pallas_call | solution.py:394
  66.3 1.6 %copy.8 = bf16[16,4096]{1,0:T(8,128)(2,1)} copy(bf16[16,4096]{1,0:T(8,128)(2,1)} %shard_map.64) | data formatting | bytes 262144
